TPU v7x, 32 devices: a whole 2x2x4 slice. The times are simulated.
32 devices in a mesh: prow: 8 (over y, x, core), pcol: 4 (over z).
Axes of the slice: x: 2, y: 2, z: 4, core: 2. Of those that a mesh axis runs over, the one named last changes fastest.
Arguments:
- ancestor_inverse: float32 [8, 8, 512, 512], P('prow', 'pcol'), may hold values from -0.09375 to 0.09375
- factor_panel: float32 [512, 8, 3, 512], P('pcol', 'prow'), may hold values from -0.75 to 0.75
- pivot_inverse: float32 [3, 512, 512], P(None, 'prow', 'pcol'), may hold values from -6 to 6
- structure: int32 [8, 3], replicated, may hold values from 0 to 1, as said below
Outputs:
- inverse_panel: float32 [512, 8, 3, 512], P('pcol', 'prow')
- diagonal_block: float32 [3, 512, 512], P(None, 'prow', 'pcol')
Inputs may be any that keep to these rules, and one draw needn't show every extreme that they name: structure[J, K] is 1 where ancestor J lies in supernode K's structure and 0 elsewhere; the last ancestor, 7, lies in every supernode's structure.
All inputs are finite; a program needn't handle non-finite values.
Results may differ from a plain program's by a relative error of at most 0.00007.
Values sent between devices are 32-bit elements; how exact they have to be, the bound alone decides.
A program may use at most 64 MiB of HBM per device.

v0:
```python
import functools

import jax
import jax.numpy as jnp
from jax import lax
from jax.experimental import pallas as pl
from jax.experimental.pallas import tpu as pltpu
from jax.sharding import PartitionSpec as P

MESH = pl.DeviceIdType.MESH
PAIR = 2
HALVES = 2


def split(value):
    high = value.astype(jnp.bfloat16)
    low = (value - high.astype(jnp.float32)).astype(jnp.bfloat16)
    return high, low


def dot3(a_high, a_low, b_high, b_low, dims):
    def one(a, b):
        return lax.dot_general(a, b, (dims, ((), ())), preferred_element_type=jnp.float32)

    return one(a_high, b_high) + (one(a_high, b_low) + one(a_low, b_high))


def kernel(
    rows_n,
    cols_n,
    struct_ref,
    factor_ref,
    inverse_ref,
    pivot_ref,
    panel_ref,
    diag_ref,
    a_full,
    a_high,
    a_low,
    staged,
    columns,
    l_high,
    l_low,
    partial,
    ring_in,
    terms,
    pair_in,
    pair_sum,
    chip_in,
    cut,
    cut_in,
    a_sem,
    hop_send,
    hop_recv,
    all_send,
    all_recv,
    ring_send,
    ring_recv,
    pair_send,
    pair_recv,
    chip_send,
    chip_recv,
    cut_send,
    cut_recv,
):
    row = lax.axis_index("prow")
    col = lax.axis_index("pcol")
    chunks = factor_ref.shape[0]
    supers = chunks // HALVES
    members, width = a_full.shape[0], a_full.shape[1]
    rows = factor_ref.shape[1]
    chips = rows_n // PAIR
    part = width // rows_n
    lanes = width // cols_n
    core = lax.rem(row, PAIR)
    chip = row // PAIR
    mate = chip * PAIR + (1 - core)
    group = row // members
    member = lax.rem(row, members)

    def wrap(value, size):
        return lax.rem(value + 4 * size, size)

    barrier = pltpu.get_barrier_semaphore()
    for step in range(1, rows_n):
        pl.semaphore_signal(
            barrier, inc=1, device_id={"prow": lax.rem(row + step, rows_n)}, device_id_type=MESH
        )
    for step in range(1, cols_n):
        pl.semaphore_signal(
            barrier, inc=1, device_id={"pcol": lax.rem(col + step, cols_n)}, device_id_type=MESH
        )
    pl.semaphore_wait(barrier, rows_n + cols_n - 2)

    def remote(src, dst, send, recv, where):
        return pltpu.make_async_remote_copy(
            src_ref=src, dst_ref=dst, send_sem=send, recv_sem=recv, device_id=where, device_id_type=MESH
        )

    class Hop:
        def __init__(self, src, dst, send, recv, where, stays):
            self.far = remote(src, dst, send, recv, where)
            self.near = pltpu.make_async_copy(src, dst, recv)
            self.stays = stays

        def start(self):
            pl.when(self.stays)(self.near.start)
            pl.when(jnp.logical_not(self.stays))(self.far.start)

        def wait_recv(self):
            pl.when(self.stays)(self.near.wait)
            pl.when(jnp.logical_not(self.stays))(self.far.wait_recv)

        def wait_send(self):
            pl.when(jnp.logical_not(self.stays))(self.far.wait_send)

    sent = []

    def across(k):
        to_group = lax.rem(group + col + k, cols_n)
        return Hop(
            factor_ref.at[k],
            staged.at[k],
            hop_send.at[0, k],
            hop_recv.at[0, k],
            {"prow": to_group * members + member},
            lax.rem(col + k, cols_n) == 0,
        )

    def along(k):
        to_col = wrap(group - col - k, cols_n)
        return Hop(
            staged.at[k],
            columns.at[k, member * cols_n + col],
            hop_send.at[1, k],
            hop_recv.at[1, k],
            {"pcol": to_col},
            to_col == col,
        )

    def arrived(k):
        to_col = wrap(group - col - k, cols_n)
        here = columns.at[k, slot_of(row, k)]
        return Hop(staged.at[k], here, hop_send.at[1, k], hop_recv.at[1, k], {"pcol": to_col}, to_col == col)

    def slot_of(source, k):
        return lax.rem(source, members) * cols_n + wrap(source // members - col - k, cols_n)

    def spread(k, index, source, target):
        here = columns.at[k, slot_of(source, k)]
        return remote(here, here, all_send.at[k, index], all_recv.at[k, index], {"prow": target})

    def back(source, step):
        return lax.rem(source - PAIR * step + rows_n, rows_n)

    def start_spread(k):
        arrived(k).wait_recv()
        for step in range(chips - 1, 0, -1):
            copy = spread(k, step, row, lax.rem(row + PAIR * step, rows_n))
            copy.start()
            sent.append(copy)
        copy = spread(k, 0, row, mate)
        copy.start()
        sent.append(copy)

    def forward(k):
        for step in range(1, chips):
            spread(k, step, back(row, step), mate).wait_recv()
            copy = spread(k, chips - 1 + step, back(row, step), mate)
            copy.start()
            sent.append(copy)

    def collect(k):
        spread(k, 0, mate, mate).wait_recv()
        for step in range(1, chips):
            spread(k, chips - 1 + step, back(mate, step), mate).wait_recv()

    def ring_block(step):
        return wrap(col - 1 - step, cols_n)

    def ring_copy(k, step):
        block = pl.ds(pl.multiple_of(ring_block(step) * rows, rows), rows)
        return remote(
            partial.at[k, block],
            ring_in.at[k, step],
            ring_send.at[k, step],
            ring_recv.at[k, step],
            {"pcol": lax.rem(col + 1, cols_n)},
        )

    def multiply(k, step):
        block = pl.ds(pl.multiple_of(ring_block(step) * rows, rows), rows)
        partial[k, block, :] = dot3(
            a_high[block, :], a_low[block, :], l_high[...], l_low[...], ((1,), (0,))
        )

    def start_ring(k):
        collect(k)

        def convert(index, carry):
            mask = struct_ref[col * members + index // cols_n, k // HALVES].astype(jnp.float32)
            high, low = split(columns[k, index] * mask)
            at = pl.ds(pl.multiple_of(index * rows, rows), rows)
            l_high[at, :] = high
            l_low[at, :] = low
            return carry

        lax.fori_loop(0, members * cols_n, convert, 0)
        multiply(k, 0)
        copy = ring_copy(k, 0)
        copy.start()
        sent.append(copy)

        def others(step, carry):
            multiply(k, step)
            return carry

        lax.fori_loop(1, cols_n, others, 0)

    def ring_step(k, step):
        ring_copy(k, step - 1).wait_recv()
        block = pl.ds(pl.multiple_of(ring_block(step) * rows, rows), rows)
        partial[k, block, :] = partial[k, block, :] + ring_in[k, step - 1]
        copy = ring_copy(k, step)
        copy.start()
        sent.append(copy)

    def pair_copy(k):
        return remote(terms.at[k, 1 - core], pair_in.at[k], pair_send.at[k], pair_recv.at[k], {"prow": mate})

    def chip_copy(k, step):
        to_chip = lax.rem(chip + step, chips)
        return remote(
            pair_sum.at[k, to_chip],
            chip_in.at[k, step - 1],
            chip_send.at[k, step - 1],
            chip_recv.at[k, step - 1],
            {"prow": to_chip * PAIR + core},
        )

    def cut_copy(k, step):
        to_col = lax.rem(col + step, cols_n)
        return remote(
            cut.at[k, to_col],
            cut_in.at[k, step - 1],
            cut_send.at[k, step - 1],
            cut_recv.at[k, step - 1],
            {"pcol": to_col},
        )

    def finish_panel(k):
        ring_copy(k, cols_n - 2).wait_recv()
        block = pl.ds(pl.multiple_of(col * rows, rows), rows)
        mask = struct_ref[row, k // HALVES].astype(jnp.float32)
        result = -mask * (partial[k, block, :] + ring_in[k, cols_n - 2])
        panel_ref[k] = result
        r_high, r_low = split(result)
        for half in range(HALVES):
            f_high, f_low = split(factor_ref[k // HALVES * HALVES + half] * mask)
            term = dot3(f_high, f_low, r_high, r_low, ((0,), (0,)))
            for here in range(rows_n // HALVES):
                at = half * (rows_n // HALVES) + here
                terms[k, at % PAIR, at // PAIR] = term[here * part : (here + 1) * part]
        copy = pair_copy(k)
        copy.start()
        sent.append(copy)

    def add_pair(k):
        pair_copy(k).wait_recv()
        pair_sum[k] = terms[k, core] + pair_in[k]
        for step in range(chips - 1, 0, -1):
            copy = chip_copy(k, step)
            copy.start()
            sent.append(copy)

    def add_chips(k):
        total = pair_sum[k, chip]
        for step in range(1, chips):
            chip_copy(k, step).wait_recv()
            total = total + chip_in[k, step - 1]
        for at in range(cols_n // HALVES):
            cut[k // HALVES, k % HALVES * (cols_n // HALVES) + at] = total[:, at * lanes : (at + 1) * lanes]
        if k % HALVES == HALVES - 1:
            for step in range(cols_n - 1, 0, -1):
                copy = cut_copy(k // HALVES, step)
                copy.start()
                sent.append(copy)

    def add_cuts(k):
        if k % HALVES < HALVES - 1:
            return
        at = k // HALVES
        total = cut[at, col]
        for step in range(1, cols_n):
            cut_copy(at, step).wait_recv()
            total = total + cut_in[at, step - 1]
        diag_ref[at] = pivot_ref[at] - total

    load = pltpu.make_async_copy(inverse_ref.at[0], a_full, a_sem)
    load.start()
    for k in range(chunks):
        across(k).start()
        sent.append(across(k))
    for k in range(chunks):
        across(k).wait_recv()
        along(k).start()
        sent.append(along(k))
    load.wait()
    for index in range(members):
        high, low = split(a_full[index])
        a_high[:, index * width : (index + 1) * width] = high
        a_low[:, index * width : (index + 1) * width] = low

    start_spread(0)
    stages = [start_ring]
    for step in range(1, cols_n - 1):
        stages.append(functools.partial(lambda at, k: ring_step(k, at), step))
    stages += [finish_panel, add_pair, add_chips, add_cuts]
    for wave in range(chunks + len(stages) - 1):
        if wave < chunks:
            if wave + 1 < chunks:
                start_spread(wave + 1)
            forward(wave)
        for k in range(chunks):
            if 0 <= wave - k < len(stages):
                stages[wave - k](k)

    for copy in sent:
        copy.wait_send()


def body(ancestor_inverse, factor_panel, pivot_inverse, structure):
    rows_n, cols_n = lax.axis_size("prow"), lax.axis_size("pcol")
    members, width = ancestor_inverse.shape[1], ancestor_inverse.shape[3]
    rows, _, supers, _ = factor_panel.shape
    chips, part, lanes = rows_n // PAIR, width // rows_n, width // cols_n
    chunks, piece = supers * HALVES, width // HALVES
    factor = jnp.transpose(factor_panel.reshape(rows, chunks, piece), (1, 0, 2))
    f32, b16, dma = jnp.float32, jnp.bfloat16, pltpu.SemaphoreType.DMA
    vmem = pl.BlockSpec(memory_space=pltpu.VMEM)
    panel, diagonal = pl.pallas_call(
        functools.partial(kernel, rows_n, cols_n),
        out_shape=(
            jax.ShapeDtypeStruct((chunks, rows, piece), f32),
            jax.ShapeDtypeStruct(pivot_inverse.shape, f32),
        ),
        in_specs=[
            pl.BlockSpec(memory_space=pltpu.SMEM),
            vmem,
            pl.BlockSpec(memory_space=pl.ANY),
            vmem,
        ],
        out_specs=(vmem, vmem),
        scratch_shapes=[
            pltpu.VMEM((members, width, width), f32),
            pltpu.VMEM((width, members * width), b16),
            pltpu.VMEM((width, members * width), b16),
            pltpu.VMEM((chunks, rows, piece), f32),
            pltpu.VMEM((chunks, members * cols_n, rows, piece), f32),
            pltpu.VMEM((members * width, piece), b16),
            pltpu.VMEM((members * width, piece), b16),
            pltpu.VMEM((chunks, width, piece), f32),
            pltpu.VMEM((chunks, cols_n - 1, rows, piece), f32),
            pltpu.VMEM((chunks, PAIR, chips, part, piece), f32),
            pltpu.VMEM((chunks, chips, part, piece), f32),
            pltpu.VMEM((chunks, chips, part, piece), f32),
            pltpu.VMEM((chunks, chips - 1, part, piece), f32),
            pltpu.VMEM((supers, cols_n, part, lanes), f32),
            pltpu.VMEM((supers, cols_n - 1, part, lanes), f32),
            dma,
            dma((2, chunks)),
            dma((2, chunks)),
            dma((chunks, 2 * chips)),
            dma((chunks, 2 * chips)),
            dma((chunks, cols_n - 1)),
            dma((chunks, cols_n - 1)),
            dma((chunks,)),
            dma((chunks,)),
            dma((chunks, chips - 1)),
            dma((chunks, chips - 1)),
            dma((supers, cols_n - 1)),
            dma((supers, cols_n - 1)),
        ],
        compiler_params=pltpu.CompilerParams(
            collective_id=0, has_side_effects=True, vmem_limit_bytes=56 * 1024 * 1024
        ),
    )(structure, factor, ancestor_inverse, pivot_inverse)
    return jnp.transpose(panel, (1, 0, 2)).reshape(factor_panel.shape), diagonal


def solution(mesh):
    placed = (
        P("prow", "pcol", None, None),
        P("pcol", "prow", None, None),
        P(None, "prow", "pcol"),
        P(),
    )
    return jax.shard_map(
        body,
        mesh=mesh,
        in_specs=placed,
        out_specs=(P("pcol", "prow", None, None), P(None, "prow", "pcol")),
        check_vma=False,
    )
```

profile of v0, /device:TPU:0, one launch (start us, length us, event | category | flops | bytes accessed | tf_op | source)
XLA Modules:
  0.0 116.8 jit_solution(9126128398416141245)
XLA Ops:
  0.6 1.3 %copy.9.struct_ref = s32[8,3]{1,0:T(8,128)} copy(s32[8,3]{0,1:T(4,128)} %param.7) | data formatting | bytes 192 | tf_op args[3]
  2.0 2.2 %copy.7 = f32[128,1,3,512]{0,3,2,1:T(8,128)S(1)} copy(f32[128,1,3,512]{3,1,2,0:T(1,128)} %param.5) | data formatting | bytes 1572864 | tf_op args[1]
  4.2 1.1 copy.8
  5.3 107.6 %shard_map.59 = (f32[6,128,256]{2,1,0:T(8,128)}, f32[3,64,128]{2,1,0:T(8,128)}) custom-call(s32[8,3]{1,0:T(8,128)} %copy.9.struct_ref, f32[6,128,256]{2,1,0:T(8,128)} %bitcast.6, f32[1,2,512,512]{3,2,1,0:T(8,128)} %inverse_ref.1, f32[3,64,128]{2,1,0:T(8,128)} %pivot_ref.1), custom_call_target="tpu_custom_call" | custom-call | tf_op jit(solution)/shard_map/pallas_call | solution.py:341
  113.0 0.0 copy-start
  113.0 1.4 %copy.10 = f32[128,6,256]{0,2,1:T(8,128)S(1)} copy(f32[128,6,256]{2,0,1:T(8,128)} %bitcast.7) | data formatting | bytes 1572864 | tf_op jit(solution)/shard_map/transpose | solution.py:388
  114.4 1.7 %copy.11 = f32[128,1,3,512]{3,1,2,0:T(1,128)} copy(f32[128,1,3,512]{0,3,2,1:T(8,128)S(1)} %bitcast.4) | data formatting | bytes 1572864
  116.1 0.0 copy-done
  116.1 0.6 copy.13
Async XLA Ops:
  113.0 3.2 %copy-start = (f32[3,64,128]{2,1,0:T(8,128)S(1)}, f32[3,64,128]{2,1,0:T(8,128)}, u32[]{:S(2)}) copy-start(f32[3,64,128]{2,1,0:T(8,128)} %get-tuple-element.11) | copy-start | bytes 294916
where the time goes:
time: 117 us
  Pallas kernels  108 us (92%)
  local copies, waits for them, and re-layouts  8.47 us (7%)
    pallas_call x1, Pallas kernels, body(): pl.pallas_call(functools.partial(kernel, rows_n, cols_n), out_shape=(jax....  108 us
    unnamed x6, local copies, waits for them, and re-layouts  5.9 us

commit v1 on v0

v1 whole, which is shorter than its diff:
```python
import functools

import jax
import jax.numpy as jnp
from jax import lax
from jax.experimental import pallas as pl
from jax.experimental.pallas import tpu as pltpu
from jax.sharding import PartitionSpec as P

MESH = pl.DeviceIdType.MESH
PAIR = 2
PIECE = 128
AHEAD = 4
LAGS = {"across": -AHEAD, "along": -3, "spread": -2, "forward": -1, "multiply": 0}
CHAIN_LAG = 1
TAIL_LAG = 1


def split(value):
    high = value.astype(jnp.bfloat16)
    low = (value - high.astype(jnp.float32)).astype(jnp.bfloat16)
    return high, low


def dot(a, b):
    return lax.dot_general(a, b, (((1,), (0,)), ((), ())), preferred_element_type=jnp.float32)


def flip(value, number, size):
    bit, total = 1, value
    while bit < size:
        if (number // bit) % 2:
            here = lax.rem(lax.div(value, bit), 2)
            total = total + bit - 2 * bit * here
        bit *= 2
    return total


def flip_both(left, right, size):
    bit, total = 1, 0
    while bit < size:
        a, b = lax.rem(lax.div(left, bit), 2), lax.rem(lax.div(right, bit), 2)
        total = total + bit * (a + b - 2 * a * b)
        bit *= 2
    return total


def kernel(
    rows_n,
    cols_n,
    struct_hbm,
    factor_hbm,
    inverse_hbm,
    pivot_ref,
    panel_hbm,
    diag_ref,
    struct,
    raw,
    a_full,
    a_high,
    a_low,
    masked,
    turned,
    staged,
    columns,
    both,
    partial,
    chain_in,
    result_out,
    terms,
    pair_in,
    pair_sum,
    chip_in,
    cut,
    cut_in,
    load_sem,
    sends,
    hop_recv,
    near_recv,
    mate_recv,
    chain_recv,
    pair_recv,
    chip_recv,
    cut_recv,
):
    row = lax.axis_index("prow")
    col = lax.axis_index("pcol")
    chunks, rows, piece = masked.shape
    members, width = a_full.shape[0], a_full.shape[1]
    supers = struct.shape[0]
    per_super = width // piece
    chips = rows_n // PAIR
    part = width // rows_n
    lanes = width // cols_n
    cuts = piece // lanes
    core = lax.rem(row, PAIR)
    chip = lax.div(row, PAIR)
    mate = chip * PAIR + (1 - core)
    group = lax.div(row, members)
    member = lax.rem(row, members)
    both_ways = flip_both(group, col, cols_n)

    load_struct = pltpu.make_async_copy(struct_hbm, struct, load_sem.at[0])
    load_raw = pltpu.make_async_copy(factor_hbm, raw, load_sem.at[1])
    load_a = pltpu.make_async_copy(inverse_hbm.at[0], a_full, load_sem.at[2])
    store_panel = pltpu.make_async_copy(result_out, panel_hbm, load_sem.at[3])
    load_struct.start()
    load_raw.start()
    load_a.start()

    barrier = pltpu.get_barrier_semaphore()
    for step in range(1, rows_n):
        pl.semaphore_signal(
            barrier, inc=1, device_id={"prow": lax.rem(row + step, rows_n)}, device_id_type=MESH
        )
    for step in range(1, cols_n):
        pl.semaphore_signal(
            barrier, inc=1, device_id={"pcol": lax.rem(col + step, cols_n)}, device_id_type=MESH
        )

    def remote(src, dst, send, recv, where):
        return pltpu.make_async_remote_copy(
            src_ref=src, dst_ref=dst, send_sem=send, recv_sem=recv, device_id=where, device_id_type=MESH
        )

    sent = []

    def begin(copy, when=None):
        if when is None:
            copy.start()
        else:
            pl.when(when)(copy.start)
        sent.append((copy, when))

    def across(k):
        to_group = flip(flip_both(group, col, cols_n), k, cols_n)
        stays = flip(col, k, cols_n) == 0
        return (
            remote(
                masked.at[k],
                staged.at[k],
                sends.at[0],
                hop_recv.at[0, k],
                {"prow": to_group * members + member},
            ),
            stays,
        )

    def start_across(k):
        mask = struct[k // per_super, row].astype(jnp.float32)
        value = raw[pl.ds(k, rows, stride=chunks), :] * mask
        masked[k] = value
        copy, stays = across(k)

        @pl.when(stays)
        def _():
            staged[k] = value

        begin(copy, jnp.logical_not(stays))

    def slot_of(source, k):
        from_col = flip(flip_both(lax.div(source, members), col, cols_n), k, cols_n)
        return lax.rem(source, members) * cols_n + from_col

    def along(k):
        to_col = flip(both_ways, k, cols_n)
        copy = remote(
            staged.at[k],
            columns.at[k, member * cols_n + col],
            sends.at[1],
            hop_recv.at[1, k],
            {"pcol": to_col},
        )
        return copy, to_col == col

    def start_along(k):
        copy, stays = across(k)
        pl.when(jnp.logical_not(stays))(copy.wait_recv)
        copy, home = along(k)

        @pl.when(home)
        def _():
            columns[k, member * cols_n + col] = staged[k]

        begin(copy, jnp.logical_not(home))

    def near(k, source, target):
        here = columns.at[k, slot_of(source, k)]
        return remote(here, here, sends.at[2], near_recv.at[k], {"prow": target})

    def over(k, source):
        here = columns.at[k, slot_of(source, k)]
        return remote(here, here, sends.at[3], mate_recv.at[k], {"prow": mate})

    def arrived(buffer, index, count, semaphore):
        here = buffer.at[index, pl.ds(0, count)]
        return remote(here, here, sends.at[0], semaphore, {"prow": mate})

    def back(source, step):
        return lax.rem(source - PAIR * step + rows_n, rows_n)

    def start_spread(k):
        copy, home = along(k)
        pl.when(jnp.logical_not(home))(copy.wait_recv)
        for step in range(chips - 1, 0, -1):
            begin(near(k, row, lax.rem(row + PAIR * step, rows_n)))
        begin(over(k, row))

    def forward(k):
        arrived(columns, k, chips - 1, near_recv.at[k]).wait_recv()
        for step in range(1, chips):
            begin(over(k, back(row, step)))

    def multiply(k):
        arrived(columns, k, chips, mate_recv.at[k]).wait_recv()
        for index in range(members * cols_n):
            high, low = split(columns[k, index])
            both[index * rows : (index + 1) * rows, :piece] = high
            both[index * rows : (index + 1) * rows, piece:] = low
        first = dot(a_high[...], both[...])
        second = dot(a_low[...], both[:, :piece])
        partial[k] = first[:, :piece] + (first[:, piece:] + second)

    def chain_copy(k, step, side):
        place = col if side == 0 else cols_n - 1 - col
        block = cols_n - 1 - step + place
        block = block if side == 0 else cols_n - 1 - block
        at = pl.ds(pl.multiple_of(block * rows, rows), rows)
        copy = remote(
            partial.at[k, at],
            chain_in.at[k, side, step],
            sends.at[4],
            chain_recv.at[k, side, step],
            {"pcol": col + 1 - 2 * side},
        )
        return copy, at, place

    def came_from(k, step, side):
        return remote(
            chain_in.at[k, side, step],
            chain_in.at[k, side, step],
            sends.at[4],
            chain_recv.at[k, side, step],
            {"pcol": lax.rem(col + 1, cols_n)},
        )

    def chain(step, k):
        for side in (0, 1):
            copy, at, place = chain_copy(k, step, side)
            if step:

                @pl.when(jnp.logical_and(place > 0, place <= step))
                def _():
                    came_from(k, step - 1, side).wait_recv()
                    partial[k, at, :] = partial[k, at, :] + chain_in[k, side, step - 1]

            begin(copy, place <= step)

    def finish_panel(k):
        own = pl.ds(pl.multiple_of(col * rows, rows), rows)
        for side in (0, 1):
            place = col if side == 0 else cols_n - 1 - col

            @pl.when(place > 0)
            def _():
                came_from(k, cols_n - 2, side).wait_recv()
                partial[k, own, :] = partial[k, own, :] + chain_in[k, side, cols_n - 2]

        mask = struct[k // per_super, row].astype(jnp.float32)
        result = -mask * partial[k, own, :]
        result_out[pl.ds(k, rows, stride=chunks), :] = result
        if k == chunks - 1:
            store_panel.start()
        high, low = split(result)
        sides = jnp.concatenate([high, low], axis=1)
        first = dot(turned[k // per_super, 0], sides)
        second = dot(turned[k // per_super, 1], high)
        term = first[:, :piece] + (first[:, piece:] + second)
        for at in range(rows_n):
            terms[k, at % PAIR, at // PAIR] = term[at * part : (at + 1) * part]
        begin(pair_copy(k))

    def pair_copy(k):
        return remote(terms.at[k, 1 - core], pair_in.at[k], sends.at[5], pair_recv.at[k], {"prow": mate})

    def chip_copy(k, step):
        to_chip = lax.rem(chip + step, chips)
        return remote(
            pair_sum.at[k, to_chip],
            chip_in.at[k, step - 1],
            sends.at[6],
            chip_recv.at[k],
            {"prow": to_chip * PAIR + core},
        )

    def add_pair(k):
        pair_copy(k).wait_recv()
        pair_sum[k] = terms[k, core] + pair_in[k]
        for step in range(chips - 1, 0, -1):
            begin(chip_copy(k, step))

    def cut_copy(k, at, target):
        step = lax.rem(col - target + cols_n, cols_n)
        return remote(
            cut.at[k, at],
            cut_in.at[k, at, step],
            sends.at[7],
            cut_recv.at[k, at],
            {"pcol": target},
        )

    def add_chips(k):
        total = pair_sum[k, chip]
        arrived(chip_in, k, chips - 1, chip_recv.at[k]).wait_recv()
        for step in range(1, chips):
            total = total + chip_in[k, step - 1]
        for at in range(cuts):
            cut[k, at] = total[:, at * lanes : (at + 1) * lanes]
            target = k % per_super * cuts + at
            begin(cut_copy(k, at, target), col != target)

    def add_cuts(k):
        for at in range(cuts):

            @pl.when(col == k % per_super * cuts + at)
            def _():
                here = cut_in.at[k, at, pl.ds(1, cols_n - 1)]
                remote(here, here, sends.at[0], cut_recv.at[k, at], {"prow": mate}).wait_recv()
                total = cut[k, at]
                for step in range(1, cols_n):
                    total = total + cut_in[k, at, step]
                diag_ref[k // per_super] = pivot_ref[k // per_super] - total

    def prepare_a():
        load_a.wait()
        for index in range(members):
            high, low = split(a_full[index])
            a_high[:, index * width : (index + 1) * width] = high
            a_low[:, index * width : (index + 1) * width] = low

    def prepare_turned(s):
        for at in range(per_super):
            high, low = split(masked[s * per_super + at].T)
            turned[s, 0, at * piece : (at + 1) * piece] = high
            turned[s, 1, at * piece : (at + 1) * piece] = low

    steps = cols_n - 1
    stages = [("add_cuts", add_cuts, CHAIN_LAG * steps + 3 * TAIL_LAG)]
    stages.append(("add_chips", add_chips, CHAIN_LAG * steps + 2 * TAIL_LAG))
    stages.append(("add_pair", add_pair, CHAIN_LAG * steps + TAIL_LAG))
    stages.append(("finish", finish_panel, CHAIN_LAG * steps))
    for step in range(steps - 1, 0, -1):
        stages.append(("chain", functools.partial(chain, step), CHAIN_LAG * step))
    stages.append(("forward", forward, LAGS["forward"]))
    stages.append(("spread", start_spread, LAGS["spread"]))
    stages.append(("along", start_along, LAGS["along"]))
    stages.append(("across", start_across, LAGS["across"]))
    stages.append(("multiply", multiply, 0))
    stages.append(("chain", functools.partial(chain, 0), 0))
    last = max(lag for _, _, lag in stages)

    load_struct.wait()
    load_raw.wait()
    pl.semaphore_wait(barrier, rows_n + cols_n - 2)

    for wave in range(-AHEAD, chunks + last):
        for _, stage, lag in stages:
            if 0 <= wave - lag < chunks:
                stage(wave - lag)
        if wave == -2:
            prepare_a()
        for s in range(supers):
            if wave + AHEAD == (s + 1) * per_super - 1:
                prepare_turned(s)

    store_panel.wait()
    for copy, when in sent:
        if when is None:
            copy.wait_send()
        else:
            pl.when(when)(copy.wait_send)


def body(ancestor_inverse, factor_panel, pivot_inverse, structure):
    rows_n, cols_n = lax.axis_size("prow"), lax.axis_size("pcol")
    members, width = ancestor_inverse.shape[1], ancestor_inverse.shape[3]
    rows, _, supers, _ = factor_panel.shape
    chips, part, lanes = rows_n // PAIR, width // rows_n, width // cols_n
    piece = max(PIECE, lanes)
    chunks, cuts = supers * width // piece, piece // lanes
    factor = factor_panel.reshape(rows * chunks, piece)
    f32, b16, dma = jnp.float32, jnp.bfloat16, pltpu.SemaphoreType.DMA
    vmem, hbm = pl.BlockSpec(memory_space=pltpu.VMEM), pl.BlockSpec(memory_space=pl.ANY)
    panel, diagonal = pl.pallas_call(
        functools.partial(kernel, rows_n, cols_n),
        out_shape=(
            jax.ShapeDtypeStruct((rows * chunks, piece), f32),
            jax.ShapeDtypeStruct(pivot_inverse.shape, f32),
        ),
        in_specs=[hbm, hbm, hbm, vmem],
        out_specs=(hbm, vmem),
        scratch_shapes=[
            pltpu.SMEM((supers, structure.shape[0]), jnp.int32),
            pltpu.VMEM((rows * chunks, piece), f32),
            pltpu.VMEM((members, width, width), f32),
            pltpu.VMEM((width, members * width), b16),
            pltpu.VMEM((width, members * width), b16),
            pltpu.VMEM((chunks, rows, piece), f32),
            pltpu.VMEM((supers, 2, width, rows), b16),
            pltpu.VMEM((chunks, rows, piece), f32),
            pltpu.VMEM((chunks, members * cols_n, rows, piece), f32),
            pltpu.VMEM((members * width, 2 * piece), b16),
            pltpu.VMEM((chunks, width, piece), f32),
            pltpu.VMEM((chunks, 2, cols_n - 1, rows, piece), f32),
            pltpu.VMEM((rows * chunks, piece), f32),
            pltpu.VMEM((chunks, PAIR, chips, part, piece), f32),
            pltpu.VMEM((chunks, chips, part, piece), f32),
            pltpu.VMEM((chunks, chips, part, piece), f32),
            pltpu.VMEM((chunks, chips - 1, part, piece), f32),
            pltpu.VMEM((chunks, cuts, part, lanes), f32),
            pltpu.VMEM((chunks, cuts, cols_n, part, lanes), f32),
            dma((4,)),
            dma((8,)),
            dma((2, chunks)),
            dma((chunks,)),
            dma((chunks,)),
            dma((chunks, 2, cols_n - 1)),
            dma((chunks,)),
            dma((chunks,)),
            dma((chunks, cuts)),
        ],
        compiler_params=pltpu.CompilerParams(
            collective_id=0, has_side_effects=True, vmem_limit_bytes=60 * 1024 * 1024
        ),
    )(structure.T, factor, ancestor_inverse, pivot_inverse)
    return panel.reshape(factor_panel.shape), diagonal


def solution(mesh):
    placed = (
        P("prow", "pcol", None, None),
        P("pcol", "prow", None, None),
        P(None, "prow", "pcol"),
        P(),
    )
    return jax.shard_map(
        body,
        mesh=mesh,
        in_specs=placed,
        out_specs=(P("pcol", "prow", None, None), P(None, "prow", "pcol")),
        check_vma=False,
    )
```

time: 117 us -> 113 us (0.966)
  local copies, waits for them, and re-layouts: 8.47 us -> 4.09 us
    unnamed x6 -> x2, local copies, waits for them, and re-layouts: 5.9 us -> 4.09 us
    transpose x1 -> x0, local copies, waits for them, and re-layouts: 1.42 us -> none  [body(): jnp.transpose(panel, (1, 0, 2)).reshape(factor_panel.shape)]
where the time goes in v1:
time: 113 us
  Pallas kernels  108 us (96%)
  local copies, waits for them, and re-layouts  4.09 us (4%)
    pallas_call x1, Pallas kernels, body(): pl.pallas_call(functools.partial(kernel, rows_n, cols_n), out_shape=(jax....  108 us
    unnamed x2, local copies, waits for them, and re-layouts  4.09 us

profile of v1, /device:TPU:0, one launch (start us, length us, event | category | flops | bytes accessed | tf_op | source)
XLA Modules:
  0.0 112.8 jit_solution(7802616110994425337)
XLA Ops:
  0.6 108.1 %shard_map.59 = (f32[1536,128]{1,0:T(8,128)}, f32[3,64,128]{2,1,0:T(8,128)}) custom-call(s32[3,8]{1,0:T(4,128)} %bitcast.5, f32[1536,128]{1,0:T(8,128)} %bitcast.4, f32[1,2,512,512]{3,2,1,0:T(8,128)} %inverse_hbm.1, f32[3,64,128]{2,1,0:T(8,128)} %pivot_ref.1), custom_call_target="tpu_custom_call" | custom-call | tf_op jit(solution)/shard_map/pallas_call | solution.py:394
  108.7 2.6 %copy.10 = f32[128,1,3,512]{3,1,2,0:T(1,128)} copy(f32[128,1,3,512]{3,1,2,0:T(1,128)} %bitcast.3) | data formatting | bytes 1572864
  111.2 1.5 %copy.11 = f32[3,64,128]{2,1,0:T(8,128)} copy(f32[3,64,128]{2,1,0:T(8,128)} %get-tuple-element.13) | data formatting | bytes 196608

commit v2 on v1

--- a/solution.py
+++ b/solution.py
@@ -10,10 +10,22 @@
 MESH = pl.DeviceIdType.MESH
 PAIR = 2
 PIECE = 128
-AHEAD = 4
-LAGS = {"across": -AHEAD, "along": -3, "spread": -2, "forward": -1, "multiply": 0}
-CHAIN_LAG = 1
-TAIL_LAG = 1
+EAGER = 5
+DIRECT = 1
+ALONG = (7.0, 1.0)
+SPREAD = (11.0, 2.4)
+RELAY = 4.0
+FORWARD = 3.5
+MULTIPLY = 2.0
+FIRST_HEAD = -1.0
+FINISH = (36.0, 3.9)
+HOP = 6.0
+LEAD = 4.0
+PAIR_TIME = 2.2
+CHIPS_TIME = 6.0
+CUTS_TIME = 12.0
+LATE_CUTS = 4
+LATE_TIME = 76.0
 
 
 def split(value):
@@ -52,7 +64,7 @@
     factor_hbm,
     inverse_hbm,
     pivot_ref,
-    panel_hbm,
+    result_out,
     diag_ref,
     struct,
     raw,
@@ -66,7 +78,6 @@
     both,
     partial,
     chain_in,
-    result_out,
     terms,
     pair_in,
     pair_sum,
@@ -77,6 +88,7 @@
     sends,
     hop_recv,
     near_recv,
+    relay_recv,
     mate_recv,
     chain_recv,
     pair_recv,
@@ -100,10 +112,18 @@
     member = lax.rem(row, members)
     both_ways = flip_both(group, col, cols_n)
 
+    def other(number):
+        return flip(chip, number, chips) * PAIR + core
+
+    besides = (other(1), other(2)) if chips == 4 else None
+    across_corner = other(3) if chips == 4 else None
+
+    def direct(k):
+        return chips != 4 or k < DIRECT
+
     load_struct = pltpu.make_async_copy(struct_hbm, struct, load_sem.at[0])
     load_raw = pltpu.make_async_copy(factor_hbm, raw, load_sem.at[1])
     load_a = pltpu.make_async_copy(inverse_hbm.at[0], a_full, load_sem.at[2])
-    store_panel = pltpu.make_async_copy(result_out, panel_hbm, load_sem.at[3])
     load_struct.start()
     load_raw.start()
     load_a.start()
@@ -202,14 +222,32 @@
     def start_spread(k):
         copy, home = along(k)
         pl.when(jnp.logical_not(home))(copy.wait_recv)
-        for step in range(chips - 1, 0, -1):
-            begin(near(k, row, lax.rem(row + PAIR * step, rows_n)))
+        if direct(k):
+            for step in range(chips - 1, 0, -1):
+                begin(near(k, row, lax.rem(row + PAIR * step, rows_n)))
+        else:
+            for beside in besides:
+                begin(near(k, row, beside))
         begin(over(k, row))
 
+    def relay(k):
+        if direct(k):
+            return
+        arrived(columns, k, 2, near_recv.at[k]).wait_recv()
+        half = rows // 2
+        for at in (0, 1):
+            here = columns.at[k, slot_of(besides[at], k), pl.ds(at * half, half)]
+            begin(remote(here, here, sends.at[2], relay_recv.at[k], {"prow": besides[1 - at]}))
+            begin(over(k, besides[at]))
+
     def forward(k):
-        arrived(columns, k, chips - 1, near_recv.at[k]).wait_recv()
-        for step in range(1, chips):
-            begin(over(k, back(row, step)))
+        if direct(k):
+            arrived(columns, k, chips - 1, near_recv.at[k]).wait_recv()
+            for step in range(1, chips):
+                begin(over(k, back(row, step)))
+        else:
+            arrived(columns, k, 1, relay_recv.at[k]).wait_recv()
+            begin(over(k, across_corner))
 
     def multiply(k):
         arrived(columns, k, chips, mate_recv.at[k]).wait_recv()
@@ -244,17 +282,22 @@
             {"pcol": lax.rem(col + 1, cols_n)},
         )
 
+    def chain_start(step, k):
+        for side in (0, 1):
+            copy, at, place = chain_copy(k, step, side)
+            begin(copy, place == 0)
+
     def chain(step, k):
         for side in (0, 1):
             copy, at, place = chain_copy(k, step, side)
-            if step:
-
-                @pl.when(jnp.logical_and(place > 0, place <= step))
-                def _():
-                    came_from(k, step - 1, side).wait_recv()
-                    partial[k, at, :] = partial[k, at, :] + chain_in[k, side, step - 1]
-
-            begin(copy, place <= step)
+            when = jnp.logical_and(place > 0, place <= step)
+
+            @pl.when(when)
+            def _():
+                came_from(k, step - 1, side).wait_recv()
+                partial[k, at, :] = partial[k, at, :] + chain_in[k, side, step - 1]
+
+            begin(copy, when)
 
     def finish_panel(k):
         own = pl.ds(pl.multiple_of(col * rows, rows), rows)
@@ -269,8 +312,6 @@
         mask = struct[k // per_super, row].astype(jnp.float32)
         result = -mask * partial[k, own, :]
         result_out[pl.ds(k, rows, stride=chunks), :] = result
-        if k == chunks - 1:
-            store_panel.start()
         high, low = split(result)
         sides = jnp.concatenate([high, low], axis=1)
         first = dot(turned[k // per_super, 0], sides)
@@ -316,6 +357,9 @@
             total = total + chip_in[k, step - 1]
         for at in range(cuts):
             cut[k, at] = total[:, at * lanes : (at + 1) * lanes]
+
+    def send_cuts(k):
+        for at in range(cuts):
             target = k % per_super * cuts + at
             begin(cut_copy(k, at, target), col != target)
 
@@ -345,35 +389,51 @@
             turned[s, 1, at * piece : (at + 1) * piece] = low
 
     steps = cols_n - 1
-    stages = [("add_cuts", add_cuts, CHAIN_LAG * steps + 3 * TAIL_LAG)]
-    stages.append(("add_chips", add_chips, CHAIN_LAG * steps + 2 * TAIL_LAG))
-    stages.append(("add_pair", add_pair, CHAIN_LAG * steps + TAIL_LAG))
-    stages.append(("finish", finish_panel, CHAIN_LAG * steps))
-    for step in range(steps - 1, 0, -1):
-        stages.append(("chain", functools.partial(chain, step), CHAIN_LAG * step))
-    stages.append(("forward", forward, LAGS["forward"]))
-    stages.append(("spread", start_spread, LAGS["spread"]))
-    stages.append(("along", start_along, LAGS["along"]))
-    stages.append(("across", start_across, LAGS["across"]))
-    stages.append(("multiply", multiply, 0))
-    stages.append(("chain", functools.partial(chain, 0), 0))
-    last = max(lag for _, _, lag in stages)
+    events = []
+
+    def plan(time, name, stage, k):
+        events.append((time, len(events), name, stage, k))
+
+    for k in range(chunks):
+        spread_time = SPREAD[0] + SPREAD[1] * k
+        forward_time = spread_time + FORWARD + RELAY
+        if direct(k):
+            forward_time += FIRST_HEAD
+        multiply_time = forward_time + MULTIPLY
+        finish_time = FINISH[0] + FINISH[1] * k
+        chips_time = finish_time + PAIR_TIME + CHIPS_TIME
+        if k == chunks - 1:
+            chips_time = finish_time + PAIR_TIME
+        plan(0.0, "across", start_across, k)
+        plan(ALONG[0] + ALONG[1] * k, "along", start_along, k)
+        plan(spread_time, "spread", start_spread, k)
+        plan(spread_time + RELAY, "relay", relay, k)
+        plan(forward_time, "forward", forward, k)
+        plan(multiply_time, "multiply", multiply, k)
+        for step in range(steps):
+            lead = LEAD * step if k >= EAGER else 0.0
+            plan(multiply_time + lead, "start", functools.partial(chain_start, step), k)
+        for step in range(1, steps):
+            chain_time = max(finish_time - HOP * (steps - step), multiply_time + HOP * step)
+            plan(chain_time, f"chain{step}", functools.partial(chain, step), k)
+        plan(finish_time, "finish", finish_panel, k)
+        plan(finish_time + PAIR_TIME, "pair", add_pair, k)
+        plan(min(chips_time, FINISH[0] + FINISH[1] * (chunks - 1) + PAIR_TIME), "chips", add_chips, k)
+        late = LATE_TIME if k >= LATE_CUTS else 0.0
+        plan(max(chips_time, late), "send", send_cuts, k)
+        plan(FINISH[0] + FINISH[1] * chunks + 100.0, "cuts", add_cuts, k)
+    for s in range(supers):
+        plan(SPREAD[0] + 0.2 + s, "turn", prepare_turned, s)
+    plan(SPREAD[0] + 0.1, "a", lambda _: prepare_a(), 0)
+    events.sort(key=lambda event: event[:2])
 
     load_struct.wait()
     load_raw.wait()
     pl.semaphore_wait(barrier, rows_n + cols_n - 2)
 
-    for wave in range(-AHEAD, chunks + last):
-        for _, stage, lag in stages:
-            if 0 <= wave - lag < chunks:
-                stage(wave - lag)
-        if wave == -2:
-            prepare_a()
-        for s in range(supers):
-            if wave + AHEAD == (s + 1) * per_super - 1:
-                prepare_turned(s)
-
-    store_panel.wait()
+    for _, _, name, stage, k in events:
+        stage(k)
+
     for copy, when in sent:
         if when is None:
             copy.wait_send()
@@ -394,11 +454,11 @@
     panel, diagonal = pl.pallas_call(
         functools.partial(kernel, rows_n, cols_n),
         out_shape=(
-            jax.ShapeDtypeStruct((rows * chunks, piece), f32),
-            jax.ShapeDtypeStruct(pivot_inverse.shape, f32),
+            pltpu.VMEM((rows * chunks, piece), f32),
+            pltpu.VMEM(pivot_inverse.shape, f32),
         ),
         in_specs=[hbm, hbm, hbm, vmem],
-        out_specs=(hbm, vmem),
+        out_specs=(vmem, vmem),
         scratch_shapes=[
             pltpu.SMEM((supers, structure.shape[0]), jnp.int32),
             pltpu.VMEM((rows * chunks, piece), f32),
@@ -412,16 +472,16 @@
             pltpu.VMEM((members * width, 2 * piece), b16),
             pltpu.VMEM((chunks, width, piece), f32),
             pltpu.VMEM((chunks, 2, cols_n - 1, rows, piece), f32),
-            pltpu.VMEM((rows * chunks, piece), f32),
             pltpu.VMEM((chunks, PAIR, chips, part, piece), f32),
             pltpu.VMEM((chunks, chips, part, piece), f32),
             pltpu.VMEM((chunks, chips, part, piece), f32),
             pltpu.VMEM((chunks, chips - 1, part, piece), f32),
             pltpu.VMEM((chunks, cuts, part, lanes), f32),
             pltpu.VMEM((chunks, cuts, cols_n, part, lanes), f32),
-            dma((4,)),
+            dma((3,)),
             dma((8,)),
             dma((2, chunks)),
+            dma((chunks,)),
             dma((chunks,)),
             dma((chunks,)),
             dma((chunks, 2, cols_n - 1)),
@@ -430,7 +490,7 @@
             dma((chunks, cuts)),
         ],
         compiler_params=pltpu.CompilerParams(
-            collective_id=0, has_side_effects=True, vmem_limit_bytes=60 * 1024 * 1024
+            collective_id=0, has_side_effects=True, vmem_limit_bytes=62 * 1024 * 1024
         ),
     )(structure.T, factor, ancestor_inverse, pivot_inverse)
     return panel.reshape(factor_panel.shape), diagonal

time: 113 us -> 93.5 us (0.83)
  Pallas kernels: 108 us -> 90.9 us
  local copies, waits for them, and re-layouts: 4.09 us -> 1.52 us
    pallas_call x1, Pallas kernels: 108 us -> 90.9 us  [body(): pl.pallas_call(functools.partial(kernel, rows_n, cols_n), out_shape=(pltp...]
    unnamed x2, local copies, waits for them, and re-layouts: 4.09 us -> 1.52 us
where the time goes in v2:
time: 93.5 us; the launch traced here: 93 us
  Pallas kernels  90.9 us (97%)
  local copies, waits for them, and re-layouts  1.52 us (2%)
    pallas_call x1, Pallas kernels, body(): pl.pallas_call(functools.partial(kernel, rows_n, cols_n), out_shape=(pltp...  90.9 us

profile of v2, /device:TPU:0, one launch (start us, length us, event | category | flops | bytes accessed | tf_op | source)
XLA Modules:
  0.0 93.0 jit_solution(17248997473922756906)
XLA Ops:
  0.6 90.9 %shard_map.59 = (f32[1536,128]{1,0:T(8,128)S(1)}, f32[3,64,128]{2,1,0:T(8,128)S(1)}) custom-call(s32[3,8]{1,0:T(4,128)} %bitcast.5, f32[1536,128]{1,0:T(8,128)} %bitcast.4, f32[1,2,512,512]{3,2,1,0:T(8,128)} %inverse_hbm.1, f32[3,64,128]{2,1,0:T(8,128)} %pivot_ref.1), custom_call_target="tpu_custom_call" | custom-call | tf_op jit(solution)/shard_map/pallas_call | solution.py:454
  91.5 0.9 copy.10
  92.4 0.6 copy.11

commit v3 on v2

--- a/solution.py
+++ b/solution.py
@@ -11,15 +11,17 @@
 PAIR = 2
 PIECE = 128
 EAGER = 5
-DIRECT = 1
-ALONG = (7.0, 1.0)
+DIRECT = 2
+BATCH = 12
+ACROSS = (4.0, 1.0)
+ALONG = (7.0, 0.6)
 SPREAD = (11.0, 2.4)
 RELAY = 4.0
 FORWARD = 3.5
 MULTIPLY = 2.0
 FIRST_HEAD = -1.0
 FINISH = (36.0, 3.9)
-HOP = 6.0
+HOP = 6.5
 LEAD = 4.0
 PAIR_TIME = 2.2
 CHIPS_TIME = 6.0
@@ -129,10 +131,12 @@
     load_a.start()
 
     barrier = pltpu.get_barrier_semaphore()
-    for step in range(1, rows_n):
-        pl.semaphore_signal(
-            barrier, inc=1, device_id={"prow": lax.rem(row + step, rows_n)}, device_id_type=MESH
-        )
+    if members == PAIR:
+        greeted = [lax.rem(row + PAIR * step, rows_n) for step in range(1, chips)] + [mate]
+    else:
+        greeted = [lax.rem(row + step, rows_n) for step in range(1, rows_n)]
+    for partner in greeted:
+        pl.semaphore_signal(barrier, inc=1, device_id={"prow": partner}, device_id_type=MESH)
     for step in range(1, cols_n):
         pl.semaphore_signal(
             barrier, inc=1, device_id={"pcol": lax.rem(col + step, cols_n)}, device_id_type=MESH
@@ -144,13 +148,15 @@
         )
 
     sent = []
-
-    def begin(copy, when=None):
+    even = chunks % cols_n == 0
+
+    def begin(copy, when=None, kept=False):
         if when is None:
             copy.start()
         else:
             pl.when(when)(copy.start)
-        sent.append((copy, when))
+        if kept:
+            sent.append((copy, when))
 
     def across(k):
         to_group = flip(flip_both(group, col, cols_n), k, cols_n)
@@ -176,7 +182,7 @@
         def _():
             staged[k] = value
 
-        begin(copy, jnp.logical_not(stays))
+        begin(copy, jnp.logical_not(stays), not even)
 
     def slot_of(source, k):
         from_col = flip(flip_both(lax.div(source, members), col, cols_n), k, cols_n)
@@ -202,7 +208,7 @@
         def _():
             columns[k, member * cols_n + col] = staged[k]
 
-        begin(copy, jnp.logical_not(home))
+        begin(copy, jnp.logical_not(home), not even)
 
     def near(k, source, target):
         here = columns.at[k, slot_of(source, k)]
@@ -404,7 +410,7 @@
         chips_time = finish_time + PAIR_TIME + CHIPS_TIME
         if k == chunks - 1:
             chips_time = finish_time + PAIR_TIME
-        plan(0.0, "across", start_across, k)
+        plan(ACROSS[0] + ACROSS[1] * k if k >= BATCH else 0.0, "across", start_across, k)
         plan(ALONG[0] + ALONG[1] * k, "along", start_along, k)
         plan(spread_time, "spread", start_spread, k)
         plan(spread_time + RELAY, "relay", relay, k)
@@ -418,27 +424,37 @@
             plan(chain_time, f"chain{step}", functools.partial(chain, step), k)
         plan(finish_time, "finish", finish_panel, k)
         plan(finish_time + PAIR_TIME, "pair", add_pair, k)
-        plan(min(chips_time, FINISH[0] + FINISH[1] * (chunks - 1) + PAIR_TIME), "chips", add_chips, k)
+        plan(min(chips_time, FINISH[0] + FINISH[1] * (chunks - 1) + PAIR_TIME + 0.1), "chips", add_chips, k)
         late = LATE_TIME if k >= LATE_CUTS else 0.0
         plan(max(chips_time, late), "send", send_cuts, k)
         plan(FINISH[0] + FINISH[1] * chunks + 100.0, "cuts", add_cuts, k)
     for s in range(supers):
-        plan(SPREAD[0] + 0.2 + s, "turn", prepare_turned, s)
+        plan(FINISH[0] - 3.0 + s, "turn", prepare_turned, s)
     plan(SPREAD[0] + 0.1, "a", lambda _: prepare_a(), 0)
     events.sort(key=lambda event: event[:2])
 
     load_struct.wait()
     load_raw.wait()
-    pl.semaphore_wait(barrier, rows_n + cols_n - 2)
+    pl.semaphore_wait(barrier, len(greeted) + cols_n - 1)
 
     for _, _, name, stage, k in events:
         stage(k)
 
+    moved = pl.ds(0, chunks - chunks // cols_n)
+    totals = [
+        (2, columns.at[:, pl.ds(0, chips - 1)]),
+        (3, columns.at[:, pl.ds(0, chips)]),
+        (4, chain_in.at[:, 0]),
+        (5, pair_in),
+        (6, chip_in),
+        (7, cut_in.at[pl.ds(0, supers), 0, pl.ds(0, cols_n - 1)]),
+    ]
+    if even:
+        totals += [(0, masked.at[moved]), (1, masked.at[moved])]
+    for kind, total in totals:
+        remote(total, total, sends.at[kind], near_recv.at[0], {"prow": mate}).wait_send()
     for copy, when in sent:
-        if when is None:
-            copy.wait_send()
-        else:
-            pl.when(when)(copy.wait_send)
+        pl.when(when)(copy.wait_send)
 
 
 def body(ancestor_inverse, factor_panel, pivot_inverse, structure):

time: 93.5 us -> 89.8 us (0.960)
  Pallas kernels: 90.9 us -> 87.5 us
    pallas_call x1, Pallas kernels: 90.9 us -> 87.5 us  [body(): pl.pallas_call(functools.partial(kernel, rows_n, cols_n), out_shape=(pltp...]
where the time goes in v3:
time: 89.8 us; the launch traced here: 89.6 us
  Pallas kernels  87.5 us (97%)
  local copies, waits for them, and re-layouts  1.52 us (2%)
    pallas_call x1, Pallas kernels, body(): pl.pallas_call(functools.partial(kernel, rows_n, cols_n), out_shape=(pltp...  87.5 us

profile of v3, /device:TPU:0, one launch (start us, length us, event | category | flops | bytes accessed | tf_op | source)
XLA Modules:
  0.0 89.6 jit_solution(17034858246249463468)
XLA Ops:
  0.6 87.5 %shard_map.59 = (f32[1536,128]{1,0:T(8,128)S(1)}, f32[3,64,128]{2,1,0:T(8,128)S(1)}) custom-call(s32[3,8]{1,0:T(4,128)} %bitcast.5, f32[1536,128]{1,0:T(8,128)} %bitcast.4, f32[1,2,512,512]{3,2,1,0:T(8,128)} %inverse_hbm.1, f32[3,64,128]{2,1,0:T(8,128)} %pivot_ref.1), custom_call_target="tpu_custom_call" | custom-call | tf_op jit(solution)/shard_map/pallas_call | solution.py:470
  88.1 0.9 copy.10
  89.0 0.6 copy.11

commit v4 on v3

--- a/solution.py
+++ b/solution.py
@@ -21,7 +21,7 @@
 MULTIPLY = 2.0
 FIRST_HEAD = -1.0
 FINISH = (36.0, 3.9)
-HOP = 6.5
+HOP = 7.0
 LEAD = 4.0
 PAIR_TIME = 2.2
 CHIPS_TIME = 6.0

time: 89.8 us -> 89.8 us (level)
  no operation moved by 1% of the time
where the time goes in v4:
time: 89.8 us; the launch traced here: 89.6 us
  Pallas kernels  87.5 us (97%)
  local copies, waits for them, and re-layouts  1.52 us (2%)
    pallas_call x1, Pallas kernels, body(): pl.pallas_call(functools.partial(kernel, rows_n, cols_n), out_shape=(pltp...  87.5 us

profile of v4, /device:TPU:0, one launch (start us, length us, event | category | flops | bytes accessed | tf_op | source)
XLA Modules:
  0.0 89.6 jit_solution(4629875919512001216)
XLA Ops:
  0.6 87.5 %shard_map.59 = (f32[1536,128]{1,0:T(8,128)S(1)}, f32[3,64,128]{2,1,0:T(8,128)S(1)}) custom-call(s32[3,8]{1,0:T(4,128)} %bitcast.5, f32[1536,128]{1,0:T(8,128)} %bitcast.4, f32[1,2,512,512]{3,2,1,0:T(8,128)} %inverse_hbm.1, f32[3,64,128]{2,1,0:T(8,128)} %pivot_ref.1), custom_call_target="tpu_custom_call" | custom-call | tf_op jit(solution)/shard_map/pallas_call | solution.py:470
  88.1 0.9 copy.10
  89.0 0.6 copy.11
